TPU v7x, 32 devices: a whole 2x2x4 slice. The times are simulated.
32 devices in a mesh: grp: 4 (over y, core), rows: 8 (over z, x).
Axes of the slice: x: 2, y: 2, z: 4, core: 2. Of those that a mesh axis runs over, the one named last changes fastest.
Arguments:
- rhs: float32 [2048, 64, 128], P(('grp', 'rows')), may hold values from -6 to 6
- fine_diag: bfloat16 [2048, 64, 64], P(('grp', 'rows')), may hold values from -0.2 to 1.2
- fine_smoother: bfloat16 [2048, 64, 64], P(('grp', 'rows')), may hold values from -4 to 4
- fine_blocks: bfloat16 [2048, 7, 64, 64], P(('grp', 'rows')), may hold values from -0.1796875 to 0.1796875
- fine_cols: int32 [2048, 7], P(('grp', 'rows')), may hold values from 0 to 2047, as said below
- aggregate: int32 [2048], P(('grp', 'rows')), may hold values from 0 to 511, as said below
- coarse_diag: bfloat16 [512, 64, 64], P('rows'), may hold values from -0.8 to 4.8
- coarse_smoother: bfloat16 [512, 64, 64], P('rows'), may hold values from -1 to 1
- coarse_blocks: bfloat16 [512, 7, 64, 64], P('rows'), may hold values from -0.71875 to 0.71875
- coarse_cols: int32 [512, 7], P('rows'), may hold values from 0 to 511, as said below
Outputs:
- solution: float32 [2048, 64, 128], P(('grp', 'rows'))
Inputs may be any that keep to these rules, and one draw needn't show every extreme that they name: fine_cols row i names rows within 32 of i; the distance 32 is reached. coarse_cols row c names rows within 32 of c; the distance 32 is reached. `aggregate`: aggregate_i lies in [r * 64, (r + 1) * 64) with r = (i // 64) mod 8.
All inputs are finite; a program needn't handle non-finite values.
Results may differ from a plain program's by a relative error of at most 0.001.
The roundings to bfloat16 on the way count: a program that leaves them out, or rounds other values in their place, can miss the bound.
Values may be sent and summed in bfloat16 or wider, within the bound.
A program may use at most 128 MiB of HBM per device.

v0:
```python
import jax
import jax.numpy as jnp
from jax import lax
from jax.sharding import PartitionSpec as P

damping = 0.8


def extended_2(cells, sides, width):
    for axis, dim in sides:
        count = lax.axis_size(axis)
        ends = count - 1
        head = lax.slice_in_dim(cells, 0, width, axis=dim)
        tail = lax.slice_in_dim(cells, cells.shape[dim] - width, cells.shape[dim], axis=dim)
        cells = jnp.concatenate(
            [
                lax.ppermute(tail, axis, [(i, (i + 1) % count) for i in range(ends)]),
                cells,
                lax.ppermute(head, axis, [((i + 1) % count, i) for i in range(ends)]),
            ],
            axis=dim,
        )
    return cells


def block_product(blocks, vector):
    return jnp.einsum(
        "nab,nbk->nak", blocks, vector.astype(jnp.bfloat16), preferred_element_type=jnp.float32
    )


def nearby_product(off_blocks, columns, extended, first_row):
    nearby = jnp.take(extended, columns - first_row, axis=0)
    return jnp.einsum("njab,njbk->nak", off_blocks, nearby, preferred_element_type=jnp.float32)


def fine_operator(fine_diag, fine_blocks, fine_cols, vector):
    rounded_rows = vector.astype(jnp.bfloat16)
    height = vector.shape[0]
    margin = height // 2
    extended = extended_2(rounded_rows, ((("grp", "rows"), 0),), margin)
    first_row = lax.axis_index(("grp", "rows")) * height - margin
    return block_product(fine_diag, rounded_rows) + nearby_product(
        fine_blocks, fine_cols, extended, first_row
    )


def coarse_nearby(off_blocks, columns, rounded_full):
    height = rounded_full.shape[0]
    margin = height // 2
    extended = extended_2(rounded_full, (("rows", 0),), margin)
    first_row = lax.axis_index("rows") * height - margin
    return nearby_product(off_blocks, columns, extended, first_row)


def on_device(
    rhs,
    fine_diag,
    fine_smoother,
    fine_blocks,
    fine_cols,
    aggregate,
    coarse_diag,
    coarse_smoother,
    coarse_blocks,
    coarse_cols,
):
    first_iterate = damping * block_product(fine_smoother, rhs)
    first_residual = rhs - fine_operator(fine_diag, fine_blocks, fine_cols, first_iterate)
    second_iterate = first_iterate + damping * block_product(fine_smoother, first_residual)
    second_residual = rhs - fine_operator(fine_diag, fine_blocks, fine_cols, second_iterate)
    coarse_height = coarse_diag.shape[0]
    local_index = aggregate - lax.axis_index("rows") * coarse_height
    selector = (local_index[:, None] == jnp.arange(coarse_height, dtype=jnp.int32)[None, :]).astype(
        jnp.float32
    )
    partial_sum = jnp.einsum(
        "fc,fak->cak", selector, second_residual, precision=lax.Precision.HIGHEST
    )
    coarse_rhs = lax.psum(partial_sum, "grp")
    coarse_first = damping * block_product(coarse_smoother, coarse_rhs)
    rounded_first = coarse_first.astype(jnp.bfloat16)
    coarse_image = block_product(coarse_diag, rounded_first) + coarse_nearby(
        coarse_blocks, coarse_cols, rounded_first
    )
    coarse_second = coarse_first + damping * block_product(
        coarse_smoother, coarse_rhs - coarse_image
    )
    return second_iterate + jnp.take(coarse_second, local_index, axis=0)


def solution(mesh):
    in_specs = (
        P(("grp", "rows"), None, None),
        P(("grp", "rows"), None, None),
        P(("grp", "rows"), None, None),
        P(("grp", "rows"), None, None, None),
        P(("grp", "rows"), None),
        P(("grp", "rows")),
        P("rows", None, None),
        P("rows", None, None),
        P("rows", None, None, None),
        P("rows", None),
    )
    out_specs = P(("grp", "rows"), None, None)
    return jax.shard_map(
        on_device, mesh=mesh, in_specs=in_specs, out_specs=out_specs, check_vma=False
    )
```

profile of v0, /device:TPU:0, one launch (start us, length us, event | category | flops | bytes accessed | tf_op | source)
XLA Modules:
  0.0 246.3 jit_solution(17737860054501911996)
XLA Ops:
  6.5 1.2 copy-done
  7.8 3.4 %multiply_convert_fusion.1 = (bf16[64,64,128]{2,1,0:T(8,128)(2,1)S(1)}, f32[64,64,128]{2,1,0:T(8,128)}) fusion(bf16[64,64,64]{2,1,0:T(8,128)(2,1)S(1)} %copy-done, f32[64,64,128]{2,1,0:T(8,128)} %param.12), kind=kOutput, calls=%fused_computation.33 | convolution fusion | flops 68681728 | bytes 5767168 | tf_op jit(solution)/shard_map/nab,nbk->nak/dot_general | solution.py:27
  11.1 1.0 fusion.39
  12.2 1.4 collective-permute-start.1
  13.6 6.3 %collective-permute-start = (bf16[32,64,128]{2,1,0:T(8,128)(2,1)}, bf16[32,64,128]{2,1,0:T(8,128)(2,1)}, u32[]{:S(2)}, u32[]{:S(2)}) collective-permute-start(bf16[32,64,128]{2,1,0:T(8,128)(2,1)} %get-tuple-element.16), channel_id=1, source_target_pairs={{0,1},{1,2},{2,3},{3,4},{4,5},{5,6},{6,7},{7,8},{8,9},{9,10},{10,1... | collective-permute-start | bytes 1572872 | tf_op jit(solution)/shard_map/ppermute | solution.py:17
  19.9 0.1 copy.18
  20.0 0.1 reshape.50
  20.1 0.1 copy.17
  20.3 1.8 fusion.43
  22.1 18.5 %collective-permute-done.1 = bf16[32,64,128]{2,1,0:T(8,128)(2,1)} collective-permute-done((bf16[32,64,128]{2,1,0:T(8,128)(2,1)}, bf16[32,64,128]{2,1,0:T(8,128)(2,1)}, u32[]{:S(2)}, u32[]{:S(2)}) %collective-permute-start.1) | collective-permute-done | bytes 524320 | tf_op jit(solution)/shard_map/ppermute | solution.py:19
  40.6 0.1 collective-permute-done
  40.7 1.8 pad_maximum_fusion
  42.4 13.3 %gather_fusion.1 = bf16[448,64,128]{2,1,0:T(8,128)(2,1)} fusion(bf16[128,64,128]{2,1,0:T(8,128)(2,1)S(1)} %pad_maximum_fusion, s32[1024]{0:T(1024)S(1)} %pad_clamp_fusion.2), kind=kCustom, calls=%fused_computation.clone | custom fusion | bytes 14681856 | tf_op jit(solution)/shard_map/jit(_take)/gather | solution.py:33
  55.8 10.1 %fusion.40 = (bf16[64,64,128]{2,1,0:T(8,128)(2,1)S(1)}, f32[64,64,128]{2,1,0:T(8,128)}) fusion(bf16[64,64,64]{2,1,0:T(8,128)(2,1)S(1)} %copy-done, f32[64,64,128]{2,1,0:T(8,128)} %param.12, f32[64,128,64]{1,2,0:T(8,128)} %fusion.43, bf16[64,7,64,64]{3,2,1,0:T(8,128)(2,1)} %param.15, bf16[64,7,64,128]{3,2,1,0:T(8,128)(2,1)} %bitcast.56, ...), kind=kOutput, calls=%fused_computation.61 | convolution fusion | flops 544210944 | bytes 20971968 | tf_op jit(solution)/shard_map/nab,nbk->nak/dot_general | solution.py:27
  65.9 0.1 fusion.38
  65.9 1.4 collective-permute-start.3
  67.4 5.2 %collective-permute-start.2 = (bf16[32,64,128]{2,1,0:T(8,128)(2,1)S(1)}, bf16[32,64,128]{2,1,0:T(8,128)(2,1)S(1)}, u32[]{:S(2)}, u32[]{:S(2)}) collective-permute-start(bf16[32,64,128]{2,1,0:T(8,128)(2,1)S(1)} %get-tuple-element.14), channel_id=1, source_target_pairs={{0,1},{1,2},{2,3},{3,4},{4,5},{5,6},{6,7},{7,8},{8,9},{9,10},{10,1... | collective-permute-start | bytes 1572872 | tf_op jit(solution)/shard_map/ppermute | solution.py:17
  72.7 1.8 fusion.44
  74.5 19.4 %collective-permute-done.3 = bf16[32,64,128]{2,1,0:T(8,128)(2,1)S(1)} collective-permute-done((bf16[32,64,128]{2,1,0:T(8,128)(2,1)S(1)}, bf16[32,64,128]{2,1,0:T(8,128)(2,1)S(1)}, u32[]{:S(2)}, u32[]{:S(2)}) %collective-permute-start.3) | collective-permute-done | bytes 524320 | tf_op jit(solution)/shard_map/ppermute | solution.py:19
  93.9 0.2 collective-permute-done.2
  94.1 1.5 pad_maximum_fusion.1
  95.5 13.3 %gather_fusion.2 = bf16[448,64,128]{2,1,0:T(8,128)(2,1)} fusion(bf16[128,64,128]{2,1,0:T(8,128)(2,1)S(1)} %pad_maximum_fusion.1, s32[1024]{0:T(1024)S(1)} %pad_clamp_fusion.2), kind=kCustom, calls=%fused_computation.1.clone | custom fusion | bytes 14681856 | tf_op jit(solution)/shard_map/jit(_take)/gather | solution.py:33
  108.9 9.2 %bitcast_subtract_fusion.1 = f32[64,64,128]{2,1,0:T(8,128)S(1)} fusion(f32[64,64,128]{2,1,0:T(8,128)} %param.12, f32[64,128,64]{1,2,0:T(8,128)} %fusion.44, bf16[64,7,64,64]{3,2,1,0:T(8,128)(2,1)} %param.15, bf16[64,7,64,128]{3,2,1,0:T(8,128)(2,1)} %bitcast.57, pred[64,7]{1,0:T(8,128)(4,1)S(1)} %copy.17), kind=kOutput, calls=%fused_computation.22 | convolution fusion | flops 474480640 | bytes 17301952 | tf_op jit(solution)/shard_map/njab,njbk->nak/dot_general | solution.py:34
  118.1 3.8 %fusion.14 = f32[64,64,128]{2,0,1:T(8,128)} fusion(f32[64,64,128]{2,1,0:T(8,128)S(1)} %bitcast_subtract_fusion.1, s32[64]{0:T(128)S(1)} %get-tuple-element.7), kind=kOutput, calls=%fused_computation.28 | convolution fusion | flops 402657280 | bytes 4194560 | tf_op jit(solution)/shard_map/fc,fak->cak/dot_general | solution.py:77
  121.9 0.0 all-reduce.2.cloned.1.call-update
  121.9 0.7 copy-done.12
  122.6 0.1 copy.24
  122.7 0.1 reshape.58
  122.8 51.9 %all-reduce.2.cloned.1.call-done = f32[64,64,128]{2,0,1:T(8,128)} async-done(((f32[64,64,128]{2,0,1:T(8,128)}), f32[64,64,128]{2,0,1:T(8,128)}) %all-reduce.2.cloned.1.call-update) | async-done | bytes 2097168 | tf_op jit(solution)/shard_map/psum | solution.py:80
  174.8 1.8 convert_element_type.29
  176.5 2.3 fusion.23
  178.8 0.3 fusion.27
  179.1 1.4 fusion.37
  180.5 1.5 collective-permute-start.5
  182.0 5.3 %collective-permute-start.4 = (bf16[32,64,128]{2,1,0:T(8,128)(2,1)}, bf16[32,64,128]{2,1,0:T(8,128)(2,1)}, u32[]{:S(2)}, u32[]{:S(2)}) collective-permute-start(bf16[32,64,128]{2,1,0:T(8,128)(2,1)} %get-tuple-element.12), channel_id=1, source_target_pairs={{0,1},{1,2},{2,3},{3,4},{4,5},{5,6},{6,7},{8,9},{9,10},{10,11},{11... | collective-permute-start | bytes 1572872 | tf_op jit(solution)/shard_map/ppermute | solution.py:17
  187.4 0.1 copy.23
  187.5 3.1 %fusion.28 = f32[64,128,64]{1,2,0:T(8,128)} fusion(bf16[64,64,64]{2,1,0:T(8,128)(2,1)} %param.18, f32[64,128,64]{1,2,0:T(8,128)S(1)} %fusion.23), kind=kOutput, calls=%fused_computation.40 | convolution fusion | flops 68157440 | bytes 4718592 | tf_op jit(solution)/shard_map/nab,nbk->nak/dot_general | solution.py:27
  190.6 5.6 %collective-permute-done.5 = bf16[32,64,128]{2,1,0:T(8,128)(2,1)} collective-permute-done((bf16[32,64,128]{2,1,0:T(8,128)(2,1)}, bf16[32,64,128]{2,1,0:T(8,128)(2,1)}, u32[]{:S(2)}, u32[]{:S(2)}) %collective-permute-start.5) | collective-permute-done | bytes 524320 | tf_op jit(solution)/shard_map/ppermute | solution.py:19
  196.1 11.1 %collective-permute-done.4 = bf16[32,64,128]{2,1,0:T(8,128)(2,1)} collective-permute-done((bf16[32,64,128]{2,1,0:T(8,128)(2,1)}, bf16[32,64,128]{2,1,0:T(8,128)(2,1)}, u32[]{:S(2)}, u32[]{:S(2)}) %collective-permute-start.4) | collective-permute-done | bytes 524320 | tf_op jit(solution)/shard_map/ppermute | solution.py:17
  207.2 1.4 pad_maximum_fusion.2
  208.7 13.3 %gather_fusion.3 = bf16[448,64,128]{2,1,0:T(8,128)(2,1)} fusion(bf16[128,64,128]{2,1,0:T(8,128)(2,1)S(1)} %pad_maximum_fusion.2, s32[1024]{0:T(1024)S(1)} %pad_clamp_fusion.1), kind=kCustom, calls=%fused_computation.2.clone | custom fusion | bytes 14681856 | tf_op jit(solution)/shard_map/jit(_take)/gather | solution.py:33
  222.1 6.8 %fusion = f32[64,128,64,1]{1,2,3,0:T(8,128)S(1)} fusion(bf16[64,7,64,64]{3,2,1,0:T(8,128)(2,1)} %param.20, bf16[64,7,64,128]{3,2,1,0:T(8,128)(2,1)} %bitcast.58, pred[64,7]{1,0:T(8,128)(4,1)S(1)} %copy.23), kind=kOutput, calls=%fused_computation.4 | convolution fusion | flops 473432064 | bytes 13107648 | tf_op jit(solution)/shard_map/njab,njbk->nak/dot_general | solution.py:34
  228.9 0.0 copy-start.10
  228.9 2.4 fusion.12
  231.3 2.6 %add_bitcast_fusion = f32[64,64,128]{2,1,0:T(8,128)} fusion(f32[64,128,64]{1,2,0:T(8,128)S(1)} %copy-done.3, bf16[64,64,64]{2,1,0:T(8,128)(2,1)S(1)} %copy-done.10, bf16[64,64,128]{2,0,1:T(8,128)(2,1)S(1)} %fusion.12), kind=kOutput, calls=%fused_computation.31 | convolution fusion | flops 68681728 | bytes 5767168 | tf_op jit(solution)/shard_map/nab,nbk->nak/dot_general | solution.py:27
  233.9 2.3 gather_fusion
  236.2 0.0 copy-start.1
  236.2 3.3 %select_add_fusion = f32[64,64,128]{2,1,0:T(8,128)} fusion(f32[64,64,128]{2,1,0:T(8,128)} %get-tuple-element.21, f32[64,64,128]{2,1,0:T(8,128)S(1)} %gather_fusion, pred[64]{0:T(512)(128)(4,1)S(1)} %get-tuple-element.6), kind=kLoop, calls=%fused_computation.30 | loop fusion | flops 1048576 | bytes 6291520 | tf_op jit(solution)/shard_map/add | solution.py:89
  (32 shorter events, 0.1 us)
Async XLA Ops:
  6.5 1.2 copy-start
  6.5 168.2 %all-reduce.2.cloned.1.call-start = ((), (), s32[]{:S(2)}) async-start(), calls=%async_computation | async-start | bytes 4194304 | tf_op jit(solution)/shard_map/psum | solution.py:80
  11.1 11.0 %copy-start.4 = (bf16[64,64,128]{2,1,0:T(8,128)(2,1)}, bf16[64,64,128]{2,1,0:T(8,128)(2,1)S(1)}, u32[]{:S(2)}) copy-start(bf16[64,64,128]{2,1,0:T(8,128)(2,1)S(1)} %get-tuple-element.18) | copy-start | bytes 3145732
  11.1 8.8 %copy-start.11 = (s32[64,7]{0,1:T(8,128)S(1)}, s32[64,7]{0,1:T(8,128)}, u32[]{:S(2)}) copy-start(s32[64,7]{0,1:T(8,128)} %param.16) | copy-start | bytes 5380
  11.1 9.1 %copy-start.8 = (bf16[64,64,64]{2,1,0:T(8,128)(2,1)S(1)}, bf16[64,64,64]{2,1,0:T(8,128)(2,1)}, u32[]{:S(2)}) copy-start(bf16[64,64,64]{2,1,0:T(8,128)(2,1)} %param.13) | copy-start | bytes 1572868
  12.2 28.5 %collective-permute-start.1 = (bf16[32,64,128]{2,1,0:T(8,128)(2,1)}, bf16[32,64,128]{2,1,0:T(8,128)(2,1)}, u32[]{:S(2)}, u32[]{:S(2)}) collective-permute-start(bf16[32,64,128]{2,1,0:T(8,128)(2,1)} %get-tuple-element.17), channel_id=1, source_target_pairs={{1,0},{2,1},{3,2},{4,3},{5,4},{6,5},{7,6},{8,7},{9,8},{10,9},{11,1... | collective-permute-start | bytes 1572872 | tf_op jit(solution)/shard_map/ppermute | solution.py:19
  13.6 27.1 %collective-permute-start = (bf16[32,64,128]{2,1,0:T(8,128)(2,1)}, bf16[32,64,128]{2,1,0:T(8,128)(2,1)}, u32[]{:S(2)}, u32[]{:S(2)}) collective-permute-start(bf16[32,64,128]{2,1,0:T(8,128)(2,1)} %get-tuple-element.16), channel_id=1, source_target_pairs={{0,1},{1,2},{2,3},{3,4},{4,5},{5,6},{6,7},{7,8},{8,9},{9,10},{10,1... | collective-permute-start | bytes 1572872 | tf_op jit(solution)/shard_map/ppermute | solution.py:17
  65.9 8.6 %copy-start.5 = (bf16[64,64,128]{2,1,0:T(8,128)(2,1)}, bf16[64,64,128]{2,1,0:T(8,128)(2,1)S(1)}, u32[]{:S(2)}) copy-start(bf16[64,64,128]{2,1,0:T(8,128)(2,1)S(1)} %get-tuple-element.20) | copy-start | bytes 3145732
  65.9 6.8 %copy-start.13 = (s32[64]{0:T(128)S(1)}, s32[64]{0:T(128)}, u32[]{:S(2)}) copy-start(s32[64]{0:T(128)} %param.17) | copy-start | bytes 772
  65.9 6.8 %copy-start.9 = (bf16[64,64,64]{2,1,0:T(8,128)(2,1)S(1)}, bf16[64,64,64]{2,1,0:T(8,128)(2,1)}, u32[]{:S(2)}) copy-start(bf16[64,64,64]{2,1,0:T(8,128)(2,1)} %param.13) | copy-start | bytes 1572868
  65.9 28.0 %collective-permute-start.3 = (bf16[32,64,128]{2,1,0:T(8,128)(2,1)S(1)}, bf16[32,64,128]{2,1,0:T(8,128)(2,1)S(1)}, u32[]{:S(2)}, u32[]{:S(2)}) collective-permute-start(bf16[32,64,128]{2,1,0:T(8,128)(2,1)S(1)} %get-tuple-element.15), channel_id=1, source_target_pairs={{1,0},{2,1},{3,2},{4,3},{5,4},{6,5},{7,6},{8,7},{9,8},{10,9},{11,1... | collective-permute-start | bytes 1572872 | tf_op jit(solution)/shard_map/ppermute | solution.py:19
  67.4 26.7 %collective-permute-start.2 = (bf16[32,64,128]{2,1,0:T(8,128)(2,1)S(1)}, bf16[32,64,128]{2,1,0:T(8,128)(2,1)S(1)}, u32[]{:S(2)}, u32[]{:S(2)}) collective-permute-start(bf16[32,64,128]{2,1,0:T(8,128)(2,1)S(1)} %get-tuple-element.14), channel_id=1, source_target_pairs={{0,1},{1,2},{2,3},{3,4},{4,5},{5,6},{6,7},{7,8},{8,9},{9,10},{10,1... | collective-permute-start | bytes 1572872 | tf_op jit(solution)/shard_map/ppermute | solution.py:17
  121.9 0.7 copy-start.12
  178.8 8.7 %copy-start.2 = (f32[64,128,64]{1,2,0:T(8,128)}, f32[64,128,64]{1,2,0:T(8,128)S(1)}, u32[]{:S(2)}) copy-start(f32[64,128,64]{1,2,0:T(8,128)S(1)} %fusion.23) | copy-start | bytes 6291460
  180.5 15.6 %collective-permute-start.5 = (bf16[32,64,128]{2,1,0:T(8,128)(2,1)}, bf16[32,64,128]{2,1,0:T(8,128)(2,1)}, u32[]{:S(2)}, u32[]{:S(2)}) collective-permute-start(bf16[32,64,128]{2,1,0:T(8,128)(2,1)} %get-tuple-element.13), channel_id=1, source_target_pairs={{1,0},{2,1},{3,2},{4,3},{5,4},{6,5},{7,6},{9,8},{10,9},{11,10},{12... | collective-permute-start | bytes 1572872 | tf_op jit(solution)/shard_map/ppermute | solution.py:19
  182.0 25.2 %collective-permute-start.4 = (bf16[32,64,128]{2,1,0:T(8,128)(2,1)}, bf16[32,64,128]{2,1,0:T(8,128)(2,1)}, u32[]{:S(2)}, u32[]{:S(2)}) collective-permute-start(bf16[32,64,128]{2,1,0:T(8,128)(2,1)} %get-tuple-element.12), channel_id=1, source_target_pairs={{0,1},{1,2},{2,3},{3,4},{4,5},{5,6},{6,7},{8,9},{9,10},{10,11},{11... | collective-permute-start | bytes 1572872 | tf_op jit(solution)/shard_map/ppermute | solution.py:17
  222.0 6.9 %copy-start.6 = (f32[64,64,128]{2,0,1:T(8,128)S(1)}, f32[64,64,128]{2,0,1:T(8,128)}, u32[]{:S(2)}) copy-start(f32[64,64,128]{2,0,1:T(8,128)} %all-reduce.2.cloned.1.call-done) | copy-start | bytes 6291460
  222.0 6.9 %copy-start.7 = (f32[64,128,64]{1,2,0:T(8,128)S(1)}, f32[64,128,64]{1,2,0:T(8,128)}, u32[]{:S(2)}) copy-start(f32[64,128,64]{1,2,0:T(8,128)} %fusion.28) | copy-start | bytes 6291460
  228.9 2.4 copy-start.3
  228.9 2.4 copy-start.10
  236.2 3.3 %copy-start.1 = (bf16[64,64,64]{2,1,0:T(8,128)(2,1)S(1)}, bf16[64,64,64]{2,1,0:T(8,128)(2,1)}, u32[]{:S(2)}) copy-start(bf16[64,64,64]{2,1,0:T(8,128)(2,1)} %param.14) | copy-start | bytes 1572868
Sparse Core Ops, SparseCore 0:
  122.0 52.6 all-reduce.1
where the time goes:
time: 247 us; the launch traced here: 246 us
  waiting for transfers between devices  107 us (43%)
  local copies, waits for them, and re-layouts  47.4 us (19%)
  matrix products  44.8 us (18%)
  starting transfers between devices  21.2 us (9%)
  between operations  13.7 us (6%)
  other arithmetic  12.4 us (5%)
    psum x1, waiting for transfers between devices, on_device(): coarse_rhs = lax.psum(partial_sum, 'grp')  51.9 us
    ppermute x3, waiting for transfers between devices, extended_2(): lax.ppermute(head, axis, [((i + 1) % count, i) for i in range(ends)])  43.5 us
    gather x3, local copies, waits for them, and re-layouts, nearby_product(): nearby = jnp.take(extended, columns - first_row, axis=0)  40 us
    dot_general x7, matrix products, block_product(): jnp.einsum('nab,nbk->nak', blocks, vector.astype(jnp.bfloat16), preferred...  25 us
    ppermute x3, starting transfers between devices, extended_2(): lax.ppermute(tail, axis, [(i, (i + 1) % count) for i in range(ends)])  16.9 us
    dot_general x2, matrix products, nearby_product(): jnp.einsum('njab,njbk->nak', off_blocks, nearby, preferred_element_type=j...  16 us
    ppermute x3, waiting for transfers between devices, extended_2(): lax.ppermute(tail, axis, [(i, (i + 1) % count) for i in range(ends)])  11.4 us
  transfers between devices with their start and end apart: 7, of which 7 were waited for; matrix products, arithmetic and copies ran while one was open for 3% of the time, Pallas kernels for 0%

commit v1 on v0

--- a/solution.py
+++ b/solution.py
@@ -77,7 +77,11 @@
     partial_sum = jnp.einsum(
         "fc,fak->cak", selector, second_residual, precision=lax.Precision.HIGHEST
     )
-    coarse_rhs = lax.psum(partial_sum, "grp")
+    coarse_rhs = partial_sum
+    for hop in (1, 2):
+        coarse_rhs = coarse_rhs + lax.ppermute(
+            coarse_rhs, "grp", [(dev, dev ^ hop) for dev in range(4)]
+        )
     coarse_first = damping * block_product(coarse_smoother, coarse_rhs)
     rounded_first = coarse_first.astype(jnp.bfloat16)
     coarse_image = block_product(coarse_diag, rounded_first) + coarse_nearby(

time: 247 us -> 233 us (0.943)
  between operations: 13.7 us -> 0.29 us
  matrix products: 44.8 us -> 42.3 us
    psum x1 -> x0, waiting for transfers between devices: 51.9 us -> none  [on_device(): coarse_rhs = lax.psum(partial_sum, 'grp')]
    ppermute x0 -> x2, waiting for transfers between devices: none -> 50.1 us  [on_device(): lax.ppermute(coarse_rhs, 'grp', [(dev, dev ^ hop) for dev in range(4)])]
  transfers between devices with their start and end apart: 7 -> 8, of which waited for: 7 -> 8; matrix products, arithmetic and copies ran while one was open for 3% -> 3% of each run, Pallas kernels for 0% -> 0%
where the time goes in v1:
time: 233 us
  waiting for transfers between devices  106 us (45%)
  local copies, waits for them, and re-layouts  46.9 us (20%)
  matrix products  42.3 us (18%)
  starting transfers between devices  23 us (10%)
  other arithmetic  14.5 us (6%)
    ppermute x2, waiting for transfers between devices, on_device(): lax.ppermute(coarse_rhs, 'grp', [(dev, dev ^ hop) for dev in range(4)])  50.1 us
    ppermute x3, waiting for transfers between devices, extended_2(): lax.ppermute(head, axis, [((i + 1) % count, i) for i in range(ends)])  43.9 us
    gather x3, local copies, waits for them, and re-layouts, nearby_product(): nearby = jnp.take(extended, columns - first_row, axis=0)  40.2 us
    dot_general x7, matrix products, block_product(): jnp.einsum('nab,nbk->nak', blocks, vector.astype(jnp.bfloat16), preferred...  23.8 us
    ppermute x3, starting transfers between devices, extended_2(): lax.ppermute(tail, axis, [(i, (i + 1) % count) for i in range(ends)])  17.2 us
    dot_general x2, matrix products, nearby_product(): jnp.einsum('njab,njbk->nak', off_blocks, nearby, preferred_element_type=j...  16 us
    ppermute x3, waiting for transfers between devices, extended_2(): lax.ppermute(tail, axis, [(i, (i + 1) % count) for i in range(ends)])  11.6 us
    convert_element_type x2, other arithmetic, block_product(): vector.astype(jnp.bfloat16)  5.82 us
  transfers between devices with their start and end apart: 8, of which 8 were waited for; matrix products, arithmetic and copies ran while one was open for 3% of the time, Pallas kernels for 0%

profile of v1, /device:TPU:0, one launch (start us, length us, event | category | flops | bytes accessed | tf_op | source)
XLA Modules:
  0.0 232.6 jit_solution(11516477134169034596)
XLA Ops:
  0.0 1.2 copy-done
  1.2 3.4 %multiply_convert_fusion.1 = (bf16[64,64,128]{2,1,0:T(8,128)(2,1)S(1)}, f32[64,64,128]{2,1,0:T(8,128)}) fusion(bf16[64,64,64]{2,1,0:T(8,128)(2,1)S(1)} %copy-done, f32[64,64,128]{2,1,0:T(8,128)} %param.12), kind=kOutput, calls=%fused_computation.33 | convolution fusion | flops 68681728 | bytes 5767168 | tf_op jit(solution)/shard_map/nab,nbk->nak/dot_general | solution.py:27
  4.6 1.0 fusion.40
  5.6 1.4 collective-permute-start.1
  7.0 6.3 %collective-permute-start = (bf16[32,64,128]{2,1,0:T(8,128)(2,1)}, bf16[32,64,128]{2,1,0:T(8,128)(2,1)}, u32[]{:S(2)}, u32[]{:S(2)}) collective-permute-start(bf16[32,64,128]{2,1,0:T(8,128)(2,1)} %get-tuple-element.18), channel_id=1, source_target_pairs={{0,1},{1,2},{2,3},{3,4},{4,5},{5,6},{6,7},{7,8},{8,9},{9,10},{10,1... | collective-permute-start | bytes 1572872 | tf_op jit(solution)/shard_map/ppermute | solution.py:17
  13.4 0.1 copy.18
  13.4 0.1 reshape.50
  13.6 0.1 copy.17
  13.7 1.8 fusion.44
  15.5 18.5 %collective-permute-done.1 = bf16[32,64,128]{2,1,0:T(8,128)(2,1)} collective-permute-done((bf16[32,64,128]{2,1,0:T(8,128)(2,1)}, bf16[32,64,128]{2,1,0:T(8,128)(2,1)}, u32[]{:S(2)}, u32[]{:S(2)}) %collective-permute-start.1) | collective-permute-done | bytes 524320 | tf_op jit(solution)/shard_map/ppermute | solution.py:19
  34.1 0.1 collective-permute-done
  34.1 1.8 pad_maximum_fusion
  35.9 13.3 %gather_fusion.1 = bf16[448,64,128]{2,1,0:T(8,128)(2,1)} fusion(bf16[128,64,128]{2,1,0:T(8,128)(2,1)S(1)} %pad_maximum_fusion, s32[1024]{0:T(1024)S(1)} %pad_clamp_fusion.2), kind=kCustom, calls=%fused_computation.clone | custom fusion | bytes 14681856 | tf_op jit(solution)/shard_map/jit(_take)/gather | solution.py:33
  49.2 10.1 %fusion.41 = (bf16[64,64,128]{2,1,0:T(8,128)(2,1)S(1)}, f32[64,64,128]{2,1,0:T(8,128)}) fusion(bf16[64,64,64]{2,1,0:T(8,128)(2,1)S(1)} %copy-done, f32[64,64,128]{2,1,0:T(8,128)} %param.12, f32[64,128,64]{1,2,0:T(8,128)} %fusion.44, bf16[64,7,64,64]{3,2,1,0:T(8,128)(2,1)} %param.15, bf16[64,7,64,128]{3,2,1,0:T(8,128)(2,1)} %bitcast.56, ...), kind=kOutput, calls=%fused_computation.62 | convolution fusion | flops 544210944 | bytes 20971968 | tf_op jit(solution)/shard_map/nab,nbk->nak/dot_general | solution.py:27
  59.3 0.1 fusion.39
  59.4 1.4 collective-permute-start.3
  60.8 5.0 %collective-permute-start.2 = (bf16[32,64,128]{2,1,0:T(8,128)(2,1)S(1)}, bf16[32,64,128]{2,1,0:T(8,128)(2,1)S(1)}, u32[]{:S(2)}, u32[]{:S(2)}) collective-permute-start(bf16[32,64,128]{2,1,0:T(8,128)(2,1)S(1)} %get-tuple-element.16), channel_id=1, source_target_pairs={{0,1},{1,2},{2,3},{3,4},{4,5},{5,6},{6,7},{7,8},{8,9},{9,10},{10,1... | collective-permute-start | bytes 1572872 | tf_op jit(solution)/shard_map/ppermute | solution.py:17
  65.9 1.8 fusion.45
  67.7 19.6 %collective-permute-done.3 = bf16[32,64,128]{2,1,0:T(8,128)(2,1)S(1)} collective-permute-done((bf16[32,64,128]{2,1,0:T(8,128)(2,1)S(1)}, bf16[32,64,128]{2,1,0:T(8,128)(2,1)S(1)}, u32[]{:S(2)}, u32[]{:S(2)}) %collective-permute-start.3) | collective-permute-done | bytes 524320 | tf_op jit(solution)/shard_map/ppermute | solution.py:19
  87.3 0.2 collective-permute-done.2
  87.5 1.5 pad_maximum_fusion.1
  89.0 13.5 %gather_fusion.2 = bf16[448,64,128]{2,1,0:T(8,128)(2,1)} fusion(bf16[128,64,128]{2,1,0:T(8,128)(2,1)S(1)} %pad_maximum_fusion.1, s32[1024]{0:T(1024)S(1)} %pad_clamp_fusion.2), kind=kCustom, calls=%fused_computation.1.clone | custom fusion | bytes 14681856 | tf_op jit(solution)/shard_map/jit(_take)/gather | solution.py:33
  102.5 9.2 %bitcast_subtract_fusion.1 = f32[64,64,128]{2,1,0:T(8,128)S(1)} fusion(f32[64,64,128]{2,1,0:T(8,128)} %param.12, f32[64,128,64]{1,2,0:T(8,128)} %fusion.45, bf16[64,7,64,64]{3,2,1,0:T(8,128)(2,1)} %param.15, bf16[64,7,64,128]{3,2,1,0:T(8,128)(2,1)} %bitcast.57, pred[64,7]{1,0:T(8,128)(4,1)S(1)} %copy.17), kind=kOutput, calls=%fused_computation.22 | convolution fusion | flops 474480640 | bytes 17301952 | tf_op jit(solution)/shard_map/njab,njbk->nak/dot_general | solution.py:34
  111.7 2.5 %fusion.14 = f32[64,64,128]{2,0,1:T(8,128)S(1)} fusion(f32[64,64,128]{2,1,0:T(8,128)S(1)} %bitcast_subtract_fusion.1, s32[64]{0:T(128)S(1)} %get-tuple-element.7), kind=kOutput, calls=%fused_computation.28 | convolution fusion | flops 402657280 | bytes 4194560 | tf_op jit(solution)/shard_map/fc,fak->cak/dot_general | solution.py:77
  114.2 0.1 collective-permute-start.4
  114.3 4.1 %collective-permute-done.4 = f32[64,64,128]{2,0,1:T(8,128)S(1)} collective-permute-done((f32[64,64,128]{2,0,1:T(8,128)S(1)}, f32[64,64,128]{2,0,1:T(8,128)S(1)}, u32[]{:S(2)}, u32[]{:S(2)}) %collective-permute-start.4) | collective-permute-done | bytes 2097184 | tf_op jit(solution)/shard_map/ppermute | solution.py:82
  118.4 0.4 add.64
  118.8 1.6 collective-permute-start.5
  120.4 0.1 copy.24
  120.5 0.1 reshape.58
  120.6 46.0 %collective-permute-done.5 = f32[64,64,128]{2,0,1:T(8,128)} collective-permute-done((f32[64,64,128]{2,0,1:T(8,128)S(1)}, f32[64,64,128]{2,0,1:T(8,128)}, u32[]{:S(2)}, u32[]{:S(2)}) %collective-permute-start.5) | collective-permute-done | bytes 2097184 | tf_op jit(solution)/shard_map/ppermute | solution.py:82
  166.7 3.5 %fusion.37 = (bf16[64,64,128]{2,0,1:T(8,128)(2,1)S(1)}, f32[64,64,128]{2,0,1:T(8,128)}) fusion(f32[64,64,128]{2,0,1:T(8,128)S(1)} %add.64, f32[64,64,128]{2,0,1:T(8,128)} %collective-permute-done.5), kind=kLoop, calls=%fused_computation.58 | loop fusion | flops 1048576 | bytes 7340032 | tf_op jit(solution)/shard_map/convert_element_type | solution.py:28
  170.1 1.2 fusion.23
  171.3 0.3 fusion.27
  171.6 1.4 fusion.38
  173.0 1.3 collective-permute-start.7
  174.2 5.8 %collective-permute-start.6 = (bf16[32,64,128]{2,1,0:T(8,128)(2,1)}, bf16[32,64,128]{2,1,0:T(8,128)(2,1)}, u32[]{:S(2)}, u32[]{:S(2)}) collective-permute-start(bf16[32,64,128]{2,1,0:T(8,128)(2,1)} %get-tuple-element.14), channel_id=1, source_target_pairs={{0,1},{1,2},{2,3},{3,4},{4,5},{5,6},{6,7},{8,9},{9,10},{10,11},{11... | collective-permute-start | bytes 1572872 | tf_op jit(solution)/shard_map/ppermute | solution.py:17
  180.1 0.1 copy.23
  180.2 3.0 %fusion.28 = f32[64,128,64]{1,2,0:T(8,128)} fusion(bf16[64,64,64]{2,1,0:T(8,128)(2,1)} %param.18, f32[64,128,64]{1,2,0:T(8,128)S(1)} %fusion.23), kind=kOutput, calls=%fused_computation.40 | convolution fusion | flops 68157440 | bytes 4718592 | tf_op jit(solution)/shard_map/nab,nbk->nak/dot_general | solution.py:27
  183.2 5.8 %collective-permute-done.7 = bf16[32,64,128]{2,1,0:T(8,128)(2,1)} collective-permute-done((bf16[32,64,128]{2,1,0:T(8,128)(2,1)}, bf16[32,64,128]{2,1,0:T(8,128)(2,1)}, u32[]{:S(2)}, u32[]{:S(2)}) %collective-permute-start.7) | collective-permute-done | bytes 524320 | tf_op jit(solution)/shard_map/ppermute | solution.py:19
  189.0 11.4 %collective-permute-done.6 = bf16[32,64,128]{2,1,0:T(8,128)(2,1)} collective-permute-done((bf16[32,64,128]{2,1,0:T(8,128)(2,1)}, bf16[32,64,128]{2,1,0:T(8,128)(2,1)}, u32[]{:S(2)}, u32[]{:S(2)}) %collective-permute-start.6) | collective-permute-done | bytes 524320 | tf_op jit(solution)/shard_map/ppermute | solution.py:17
  200.4 1.4 pad_maximum_fusion.2
  201.8 13.3 %gather_fusion.3 = bf16[448,64,128]{2,1,0:T(8,128)(2,1)} fusion(bf16[128,64,128]{2,1,0:T(8,128)(2,1)S(1)} %pad_maximum_fusion.2, s32[1024]{0:T(1024)S(1)} %pad_clamp_fusion.1), kind=kCustom, calls=%fused_computation.2.clone | custom fusion | bytes 14681856 | tf_op jit(solution)/shard_map/jit(_take)/gather | solution.py:33
  215.2 6.8 %fusion = f32[64,128,64,1]{1,2,3,0:T(8,128)S(1)} fusion(bf16[64,7,64,64]{3,2,1,0:T(8,128)(2,1)} %param.20, bf16[64,7,64,128]{3,2,1,0:T(8,128)(2,1)} %bitcast.58, pred[64,7]{1,0:T(8,128)(4,1)S(1)} %copy.23), kind=kOutput, calls=%fused_computation.4 | convolution fusion | flops 473432064 | bytes 13107648 | tf_op jit(solution)/shard_map/njab,njbk->nak/dot_general | solution.py:34
  222.1 2.4 %fusion.12 = bf16[64,64,128]{2,0,1:T(8,128)(2,1)S(1)} fusion(f32[64,64,128]{2,0,1:T(8,128)S(1)} %copy-done.6, f32[64,128,64,1]{1,2,3,0:T(8,128)S(1)} %fusion, f32[64,128,64]{1,2,0:T(8,128)S(1)} %copy-done.7), kind=kLoop, calls=%fused_computation.20 | loop fusion | flops 1572864 | bytes 7340032 | tf_op jit(solution)/shard_map/convert_element_type | solution.py:28
  224.4 2.6 %add_bitcast_fusion = f32[64,64,128]{2,1,0:T(8,128)} fusion(f32[64,128,64]{1,2,0:T(8,128)S(1)} %copy-done.3, bf16[64,64,64]{2,1,0:T(8,128)(2,1)S(1)} %copy-done.11, bf16[64,64,128]{2,0,1:T(8,128)(2,1)S(1)} %fusion.12), kind=kOutput, calls=%fused_computation.31 | convolution fusion | flops 68681728 | bytes 5767168 | tf_op jit(solution)/shard_map/nab,nbk->nak/dot_general | solution.py:27
  227.0 2.3 gather_fusion
  229.3 3.3 %select_add_fusion = f32[64,64,128]{2,1,0:T(8,128)} fusion(f32[64,64,128]{2,1,0:T(8,128)} %get-tuple-element.23, f32[64,64,128]{2,1,0:T(8,128)S(1)} %gather_fusion, pred[64]{0:T(512)(128)(4,1)S(1)} %get-tuple-element.6), kind=kLoop, calls=%fused_computation.30 | loop fusion | flops 1048576 | bytes 6291520 | tf_op jit(solution)/shard_map/add | solution.py:93
  (36 shorter events, 0.1 us)
Async XLA Ops:
  0.0 1.2 copy-start
  4.6 11.0 %copy-start.4 = (bf16[64,64,128]{2,1,0:T(8,128)(2,1)}, bf16[64,64,128]{2,1,0:T(8,128)(2,1)S(1)}, u32[]{:S(2)}) copy-start(bf16[64,64,128]{2,1,0:T(8,128)(2,1)S(1)} %get-tuple-element.20) | copy-start | bytes 3145732
  4.6 8.8 %copy-start.12 = (s32[64,7]{0,1:T(8,128)S(1)}, s32[64,7]{0,1:T(8,128)}, u32[]{:S(2)}) copy-start(s32[64,7]{0,1:T(8,128)} %param.16) | copy-start | bytes 5380
  4.6 9.1 %copy-start.8 = (bf16[64,64,64]{2,1,0:T(8,128)(2,1)S(1)}, bf16[64,64,64]{2,1,0:T(8,128)(2,1)}, u32[]{:S(2)}) copy-start(bf16[64,64,64]{2,1,0:T(8,128)(2,1)} %param.13) | copy-start | bytes 1572868
  5.6 28.5 %collective-permute-start.1 = (bf16[32,64,128]{2,1,0:T(8,128)(2,1)}, bf16[32,64,128]{2,1,0:T(8,128)(2,1)}, u32[]{:S(2)}, u32[]{:S(2)}) collective-permute-start(bf16[32,64,128]{2,1,0:T(8,128)(2,1)} %get-tuple-element.19), channel_id=1, source_target_pairs={{1,0},{2,1},{3,2},{4,3},{5,4},{6,5},{7,6},{8,7},{9,8},{10,9},{11,1... | collective-permute-start | bytes 1572872 | tf_op jit(solution)/shard_map/ppermute | solution.py:19
  7.0 27.1 %collective-permute-start = (bf16[32,64,128]{2,1,0:T(8,128)(2,1)}, bf16[32,64,128]{2,1,0:T(8,128)(2,1)}, u32[]{:S(2)}, u32[]{:S(2)}) collective-permute-start(bf16[32,64,128]{2,1,0:T(8,128)(2,1)} %get-tuple-element.18), channel_id=1, source_target_pairs={{0,1},{1,2},{2,3},{3,4},{4,5},{5,6},{6,7},{7,8},{8,9},{9,10},{10,1... | collective-permute-start | bytes 1572872 | tf_op jit(solution)/shard_map/ppermute | solution.py:17
  59.3 8.4 %copy-start.5 = (bf16[64,64,128]{2,1,0:T(8,128)(2,1)}, bf16[64,64,128]{2,1,0:T(8,128)(2,1)S(1)}, u32[]{:S(2)}) copy-start(bf16[64,64,128]{2,1,0:T(8,128)(2,1)S(1)} %get-tuple-element.22) | copy-start | bytes 3145732
  59.3 6.6 %copy-start.14 = (s32[64]{0:T(128)S(1)}, s32[64]{0:T(128)}, u32[]{:S(2)}) copy-start(s32[64]{0:T(128)} %param.17) | copy-start | bytes 772
  59.3 6.6 %copy-start.9 = (bf16[64,64,64]{2,1,0:T(8,128)(2,1)S(1)}, bf16[64,64,64]{2,1,0:T(8,128)(2,1)}, u32[]{:S(2)}) copy-start(bf16[64,64,64]{2,1,0:T(8,128)(2,1)} %param.13) | copy-start | bytes 1572868
  59.4 28.0 %collective-permute-start.3 = (bf16[32,64,128]{2,1,0:T(8,128)(2,1)S(1)}, bf16[32,64,128]{2,1,0:T(8,128)(2,1)S(1)}, u32[]{:S(2)}, u32[]{:S(2)}) collective-permute-start(bf16[32,64,128]{2,1,0:T(8,128)(2,1)S(1)} %get-tuple-element.17), channel_id=1, source_target_pairs={{1,0},{2,1},{3,2},{4,3},{5,4},{6,5},{7,6},{8,7},{9,8},{10,9},{11,1... | collective-permute-start | bytes 1572872 | tf_op jit(solution)/shard_map/ppermute | solution.py:19
  60.8 26.7 %collective-permute-start.2 = (bf16[32,64,128]{2,1,0:T(8,128)(2,1)S(1)}, bf16[32,64,128]{2,1,0:T(8,128)(2,1)S(1)}, u32[]{:S(2)}, u32[]{:S(2)}) collective-permute-start(bf16[32,64,128]{2,1,0:T(8,128)(2,1)S(1)} %get-tuple-element.16), channel_id=1, source_target_pairs={{0,1},{1,2},{2,3},{3,4},{4,5},{5,6},{6,7},{7,8},{8,9},{9,10},{10,1... | collective-permute-start | bytes 1572872 | tf_op jit(solution)/shard_map/ppermute | solution.py:17
  114.2 6.2 %copy-start.13 = (s32[64,7]{0,1:T(8,128)S(1)}, s32[64,7]{0,1:T(8,128)}, u32[]{:S(2)}) copy-start(s32[64,7]{0,1:T(8,128)} %param.21) | copy-start | bytes 5380
  114.2 4.2 %collective-permute-start.4 = (f32[64,64,128]{2,0,1:T(8,128)S(1)}, f32[64,64,128]{2,0,1:T(8,128)S(1)}, u32[]{:S(2)}, u32[]{:S(2)}) collective-permute-start(f32[64,64,128]{2,0,1:T(8,128)S(1)} %fusion.14), channel_id=1, source_target_pairs={{0,8},{8,0},{16,24},{24,16},{1,9},{9,1},{17,25},{25,17},{2,10},{10... | collective-permute-start | bytes 6291464 | tf_op jit(solution)/shard_map/ppermute | solution.py:82
  118.8 47.8 %collective-permute-start.5 = (f32[64,64,128]{2,0,1:T(8,128)S(1)}, f32[64,64,128]{2,0,1:T(8,128)}, u32[]{:S(2)}, u32[]{:S(2)}) collective-permute-start(f32[64,64,128]{2,0,1:T(8,128)S(1)} %add.64), channel_id=1, source_target_pairs={{0,16},{8,24},{16,0},{24,8},{1,17},{9,25},{17,1},{25,9},{2,18},{10... | collective-permute-start | bytes 6291464 | tf_op jit(solution)/shard_map/ppermute | solution.py:82
  120.6 49.5 %copy-start.10 = (bf16[64,64,64]{2,1,0:T(8,128)(2,1)S(1)}, bf16[64,64,64]{2,1,0:T(8,128)(2,1)}, u32[]{:S(2)}) copy-start(bf16[64,64,64]{2,1,0:T(8,128)(2,1)} %param.19) | copy-start | bytes 1572868
  171.3 8.9 %copy-start.2 = (f32[64,128,64]{1,2,0:T(8,128)}, f32[64,128,64]{1,2,0:T(8,128)S(1)}, u32[]{:S(2)}) copy-start(f32[64,128,64]{1,2,0:T(8,128)S(1)} %fusion.23) | copy-start | bytes 6291460
  173.0 16.0 %collective-permute-start.7 = (bf16[32,64,128]{2,1,0:T(8,128)(2,1)}, bf16[32,64,128]{2,1,0:T(8,128)(2,1)}, u32[]{:S(2)}, u32[]{:S(2)}) collective-permute-start(bf16[32,64,128]{2,1,0:T(8,128)(2,1)} %get-tuple-element.15), channel_id=1, source_target_pairs={{1,0},{2,1},{3,2},{4,3},{5,4},{6,5},{7,6},{9,8},{10,9},{11,10},{12... | collective-permute-start | bytes 1572872 | tf_op jit(solution)/shard_map/ppermute | solution.py:19
  174.2 26.1 %collective-permute-start.6 = (bf16[32,64,128]{2,1,0:T(8,128)(2,1)}, bf16[32,64,128]{2,1,0:T(8,128)(2,1)}, u32[]{:S(2)}, u32[]{:S(2)}) collective-permute-start(bf16[32,64,128]{2,1,0:T(8,128)(2,1)} %get-tuple-element.14), channel_id=1, source_target_pairs={{0,1},{1,2},{2,3},{3,4},{4,5},{5,6},{6,7},{8,9},{9,10},{10,11},{11... | collective-permute-start | bytes 1572872 | tf_op jit(solution)/shard_map/ppermute | solution.py:17
  215.2 6.9 %copy-start.6 = (f32[64,64,128]{2,0,1:T(8,128)S(1)}, f32[64,64,128]{2,0,1:T(8,128)}, u32[]{:S(2)}) copy-start(f32[64,64,128]{2,0,1:T(8,128)} %get-tuple-element.11) | copy-start | bytes 6291460
  215.2 6.9 %copy-start.7 = (f32[64,128,64]{1,2,0:T(8,128)S(1)}, f32[64,128,64]{1,2,0:T(8,128)}, u32[]{:S(2)}) copy-start(f32[64,128,64]{1,2,0:T(8,128)} %fusion.28) | copy-start | bytes 6291460
  222.0 2.4 %copy-start.3 = (f32[64,128,64]{1,2,0:T(8,128)S(1)}, f32[64,128,64]{1,2,0:T(8,128)}, u32[]{:S(2)}) copy-start(f32[64,128,64]{1,2,0:T(8,128)} %copy-done.2) | copy-start | bytes 6291460
  222.1 2.4 %copy-start.11 = (bf16[64,64,64]{2,1,0:T(8,128)(2,1)S(1)}, bf16[64,64,64]{2,1,0:T(8,128)(2,1)}, u32[]{:S(2)}) copy-start(bf16[64,64,64]{2,1,0:T(8,128)(2,1)} %param.19) | copy-start | bytes 1572868
  229.3 3.3 %copy-start.1 = (bf16[64,64,64]{2,1,0:T(8,128)(2,1)S(1)}, bf16[64,64,64]{2,1,0:T(8,128)(2,1)}, u32[]{:S(2)}) copy-start(bf16[64,64,64]{2,1,0:T(8,128)(2,1)} %param.14) | copy-start | bytes 1572868
